TPU v7x, 32 devices: a whole 2x2x4 slice. The times are simulated.
32 devices in a mesh: head: 8 (over z, x), client: 4 (over y, core).
Axes of the slice: x: 2, y: 2, z: 4, core: 2. Of those that a mesh axis runs over, the one named last changes fastest.
Arguments:
- client_ids: int32 [32], replicated, may hold values from 0 to 127, as said below
- client_table: bfloat16 [128, 256], replicated, may hold values from -6 to 6
- in_weight: bfloat16 [256, 4096], P(None, 'client'), may hold values from -0.375 to 0.375
- in_bias: float32 [4096], P('client'), may hold values from -3 to 3
- head_weight: bfloat16 [4096, 131072], P('client', 'head'), may hold values from -0.09375 to 0.09375
- tokens: int32 [32, 256], P(('head', 'client')), may hold values from 0 to 255
- labels: int32 [32, 256], P(('head', 'client')), may hold values from 0 to 255
- byte_table: bfloat16 [256, 4096], P(None, 'client'), may hold values from -5.5 to 6.7
- out_table: bfloat16 [256, 4096], P(None, 'client'), may hold values from -5.625 to 5.625
Outputs:
- head_grad: bfloat16 [4096, 131072], P('client', 'head')
- in_grad: float32 [256, 4096], P(None, 'client')
- losses: float32 [32], P(('head', 'client'))
Inputs may be any that keep to these rules, and one draw needn't show every extreme that they name: `client_ids`: distinct population indices.
All inputs are finite; a program needn't handle non-finite values.
Results may differ from a plain program's by a relative error of at most 0.0085.
Values may be sent and summed in bfloat16 or wider, within the bound.
A program may use at most 128 MiB of HBM per device.

v0:
```python
import jax
import jax.numpy as jnp
from jax import lax
from jax.sharding import PartitionSpec as P

EPSILON = 1e-06
learn_rate = 0.1


def client_loss(factor_a, factor_b, inputs, label_row, out_table):
    depth = factor_a.shape[0]
    rank_size = factor_a.shape[1]
    normed_in = inputs * lax.rsqrt(jnp.mean(inputs * inputs, -1, keepdims=True) + EPSILON)
    low_rank = jnp.dot(normed_in, factor_a, precision=lax.Precision.HIGHEST)
    adapted = inputs + jnp.dot(low_rank, factor_b, precision=lax.Precision.HIGHEST) / jnp.sqrt(
        jnp.float32(depth * rank_size)
    )
    normed = (adapted * lax.rsqrt(jnp.mean(adapted * adapted, -1, keepdims=True) + EPSILON)).astype(
        jnp.bfloat16
    )
    logits = lax.dot_general(
        normed, out_table, (((1,), (1,)), ((), ())), preferred_element_type=jnp.float32
    )
    logits = logits * (4.0 / jnp.sqrt(jnp.float32(depth)))
    log_total = jax.nn.logsumexp(logits, -1)
    vocab_ids = lax.broadcasted_iota(jnp.int32, logits.shape, 1)
    picked = jnp.sum(jnp.where(vocab_ids == label_row[:, None], logits, 0.0), -1)
    return jnp.sum(log_total - picked)


def train_client(factor_row, token_row, label_row, byte_table, out_table):
    depth = byte_table.shape[1]
    split_at = factor_row.shape[0] // 2
    rank_size = split_at // depth
    start_a = factor_row[:split_at].reshape(depth, rank_size).astype(jnp.float32)
    start_b = factor_row[split_at:].reshape(rank_size, depth).astype(jnp.float32)
    onehot = (
        token_row[:, None]
        == lax.broadcasted_iota(jnp.int32, (token_row.shape[0], byte_table.shape[0]), 1)
    ).astype(jnp.bfloat16)
    inputs = jnp.dot(onehot, byte_table, preferred_element_type=jnp.float32)
    loss_grad = jax.value_and_grad(client_loss, argnums=(0, 1))
    first_loss, (grad_a, grad_b) = loss_grad(start_a, start_b, inputs, label_row, out_table)
    middle_a = start_a - learn_rate * grad_a
    middle_b = start_b - learn_rate * grad_b
    second_loss, (grad_a, grad_b) = loss_grad(middle_a, middle_b, inputs, label_row, out_table)
    final_a = middle_a - learn_rate * grad_a
    final_b = middle_b - learn_rate * grad_b
    deltas = jnp.concatenate(
        [(final_a - start_a).reshape(-1), (final_b - start_b).reshape(-1)]
    ).astype(jnp.bfloat16)
    return (deltas, first_loss / token_row.shape[0])


def local(
    client_ids, client_table, in_weight, in_bias, head_weight, tokens, labels, byte_table, out_table
):
    head_count = lax.axis_size("head")
    group_count = lax.axis_size("client")
    per_device = tokens.shape[0]
    byte_full, out_full = (
        lax.all_gather(byte_table, "client", axis=1, tiled=True),
        lax.all_gather(out_table, "client", axis=1, tiled=True),
    )
    ordered = client_ids.reshape(head_count, group_count, per_device).transpose(1, 0, 2).reshape(-1)
    chosen = client_table[ordered]
    preact = jnp.dot(chosen, in_weight, preferred_element_type=jnp.float32) + in_bias
    hidden = jnp.maximum(preact, 0.0).astype(jnp.bfloat16)
    hidden_rows = hidden
    summed = lax.psum_scatter(
        jnp.dot(hidden_rows, head_weight, preferred_element_type=jnp.float32),
        "client",
        scatter_dimension=0,
        tiled=True,
    )
    owned = lax.all_to_all(
        summed.astype(jnp.bfloat16), "head", split_axis=0, concat_axis=1, tiled=True
    )

    def run_client(record):
        return train_client(record[0], record[1], record[2], byte_full, out_full)

    deltas, losses = lax.map(run_client, (owned, tokens, labels))
    returned = lax.all_to_all(deltas, "head", split_axis=1, concat_axis=0, tiled=True)
    received = lax.all_gather(returned, "client", axis=0, tiled=True)
    hidden_rows = hidden
    grad_sum = lax.dot_general(
        hidden_rows, received, (((0,), (0,)), ((), ())), preferred_element_type=jnp.float32
    )
    partial_value = lax.dot_general(
        received, head_weight, (((1,), (1,)), ((), ())), preferred_element_type=jnp.float32
    )
    hidden_back = partial_value
    grad_sum, hidden_back = (grad_sum, hidden_back)
    hidden_back = lax.psum(hidden_back, "head")
    masked = jnp.where(preact > 0, hidden_back, 0.0)
    in_grad = lax.dot_general(
        chosen.astype(jnp.float32),
        masked,
        (((0,), (0,)), ((), ())),
        precision=lax.Precision.HIGHEST,
    )
    return (grad_sum.astype(jnp.bfloat16), in_grad, losses)


def solution(mesh):
    placed = (
        P(),
        P(),
        P(None, "client"),
        P("client"),
        P("client", "head"),
        P(("head", "client"), None),
        P(("head", "client"), None),
        P(None, "client"),
        P(None, "client"),
    )
    return jax.shard_map(
        local,
        mesh=mesh,
        in_specs=placed,
        out_specs=(P("client", "head"), P(None, "client"), P(("head", "client"))),
        check_vma=False,
    )
```

profile of v0, /device:TPU:0, one launch (start us, length us, event | category | flops | bytes accessed | tf_op | source)
XLA Modules:
  0.0 274.1 jit_solution(7337150185194927193)
XLA Ops:
  10.5 14.9 %fusion.59 = f32[32,16384]{1,0:T(8,128)} fusion(bf16[1024,16384]{1,0:T(8,128)(2,1)} %param.13, f32[32,1024]{1,0:T(8,128)S(1)} %convolution_add_fusion), kind=kOutput, calls=%fused_computation.91 | convolution fusion | flops 1073807360 | bytes 35782656 | tf_op jit(solution)/shard_map/dot_general | solution.py:71
  26.9 32.6 %reduce-scatter.2.cloned.1.call-done = f32[8,16384]{1,0:T(8,128)} async-done(((f32[32,16384]{1,0:T(8,128)}), f32[8,16384]{1,0:T(8,128)}) %reduce-scatter.2.cloned.1.call-update) | async-done | bytes 524304 | tf_op jit(solution)/shard_map/reduce_scatter | solution.py:70
  62.8 5.5 %all-to-all-start = ((bf16[8,2,8192]{2,1,0:T(2,128)(2,1)}), bf16[8,2,8192]{2,1,0:T(2,128)(2,1)S(1)}, u32[]{:S(2)}, u32[]{:S(2)}) async-start(bf16[8,2,8192]{2,1,0:T(2,128)(2,1)} %reshape.181), calls=%async_computation.1 | async-start | bytes 524288 | tf_op jit(solution)/shard_map/all_to_all | solution.py:76
  68.3 15.3 %all-gather.5.cloned.1.call-done = bf16[256,4096]{1,0:T(8,128)(2,1)} async-done(((bf16[256,1024]{1,0:T(8,128)(2,1)}), bf16[256,4096]{1,0:T(8,128)(2,1)}) %all-gather.5.cloned.1.call-update) | async-done | bytes 2097168 | tf_op jit(solution)/shard_map/all_gather | solution.py:62
  83.7 4.4 %multiply_reduce_fusion.2 = (f32[256]{0:T(256)S(1)}, f32[256,4096]{1,0:T(8,128)}) fusion(bf16[256,4096]{1,0:T(8,128)(2,1)} %all-gather.5.cloned.1.call-done, s32[256]{0:T(256)S(1)} %bitcast.43), kind=kOutput, calls=%fused_computation.34 | convolution fusion | flops 539033344 | bytes 6293504 | tf_op jit(solution)/shard_map/while/body/eval_jaxpr/dot_general | solution.py:41
  91.2 5.0 %fusion.18 = f32[256,16]{0,1:T(8,128)S(1)} fusion(bf16[4096,16]{1,0:T(8,128)(2,1)S(1)} %reshape.168, f32[256,4096]{1,0:T(8,128)} %get-tuple-element.34, f32[256]{0:T(256)S(1)} %add_rsqrt_fusion), kind=kOutput, calls=%fused_computation.39 | convolution fusion | flops 202375168 | bytes 4342784 | tf_op jit(solution)/shard_map/while/body/eval_jaxpr/jvp()/dot_general | solution.py:14
  96.3 4.3 %multiply_reduce_fusion.1 = (f32[256]{0:T(256)S(1)}, f32[256,4096]{1,0:T(8,128)}) fusion(f32[256,4096]{1,0:T(8,128)S(1)} %copy-done.2, f32[256,16]{0,1:T(8,128)S(1)} %fusion.18, bf16[16,4096]{1,0:T(8,128)(2,1)S(1)} %reshape.169), kind=kOutput, calls=%fused_computation.33 | convolution fusion | flops 205520640 | bytes 8537088 | tf_op jit(solution)/shard_map/while/body/eval_jaxpr/jvp()/dot_general | solution.py:15
  100.6 7.2 %all-gather.7.cloned.1.call-done = bf16[256,4096]{1,0:T(8,128)(2,1)} async-done(((bf16[256,1024]{1,0:T(8,128)(2,1)}), bf16[256,4096]{1,0:T(8,128)(2,1)}) %all-gather.7.cloned.1.call-update) | async-done | bytes 2097168 | tf_op jit(solution)/shard_map/all_gather | solution.py:63
  107.8 3.9 %fusion.78 = (f32[256]{0:T(256)S(1)}, f32[256,256]{0,1:T(8,128)S(1)}) fusion(bf16[256,4096]{1,0:T(8,128)(2,1)} %all-gather.7.cloned.1.call-done, f32[256,4096]{1,0:T(8,128)} %get-tuple-element.36, f32[256]{0:T(256)S(1)} %fusion.60), kind=kOutput, calls=%fused_computation.118 | convolution fusion | flops 539098880 | bytes 6555648 | tf_op jit(solution)/shard_map/while/body/eval_jaxpr/jvp()/dot_general | solution.py:21
  113.5 2.8 %fusion.76 = f32[256,16]{0,1:T(8,128)S(1)} fusion(bf16[16,4096]{1,0:T(8,128)(2,1)S(1)} %reshape.169, bf16[256,4096]{1,0:T(8,128)(2,1)S(1)} %get-tuple-element.40, f32[256,4096]{1,0:T(8,128)S(1)} %copy-done.4, f32[256]{0:T(256)S(1)} %multiply_multiply_fusion.1, f32[256]{0:T(256)S(1)} %fusion.60), kind=kOutput, calls=%fused_computation.117 | convolution fusion | flops 207618048 | bytes 6440960 | tf_op jit(solution)/shard_map/while/body/eval_jaxpr/transpose(jvp())/dot_general | solution.py:15
  116.3 3.1 %fusion.6 = f32[16,4096]{1,0:T(8,128)S(1)} fusion(f32[256,16]{0,1:T(8,128)S(1)} %fusion.18, bf16[16,4096]{1,0:T(8,128)(2,1)S(1)} %reshape.169, bf16[256,4096]{1,0:T(8,128)(2,1)S(1)} %get-tuple-element.40, f32[256,4096]{1,0:T(8,128)S(1)} %copy-done.4, f32[256]{0:T(256)S(1)} %multiply_multiply_fusion.1, f32[256]{0:T(256)S(1)} %fusion.60), kind=kOutput, calls=%fused_computation.21 | convolution fusion | flops 207814656 | bytes 6703104 | tf_op jit(solution)/shard_map/while/body/eval_jaxpr/transpose(jvp())/dot_general | solution.py:15
  119.4 2.5 fusion.7
  121.9 3.4 %fusion.15 = f32[256,16]{0,1:T(8,128)S(1)} fusion(f32[4096,16]{0,1:T(8,128)S(1)} %fusion.7, f32[256,4096]{1,0:T(8,128)S(1)} %copy-done.3, f32[256]{0:T(256)S(1)} %add_rsqrt_fusion), kind=kOutput, calls=%fused_computation.36 | convolution fusion | flops 202375168 | bytes 4473856 | tf_op jit(solution)/shard_map/while/body/eval_jaxpr/jvp()/dot_general | solution.py:14
  125.4 4.1 %multiply_reduce_fusion = (f32[256]{0:T(256)S(1)}, f32[256,4096]{1,0:T(8,128)S(1)}) fusion(f32[256,4096]{1,0:T(8,128)S(1)} %copy-done.3, f32[256,16]{0,1:T(8,128)S(1)} %fusion.15, f32[16,4096]{1,0:T(8,128)S(1)} %fusion.6), kind=kOutput, calls=%fused_computation.31 | convolution fusion | flops 205520640 | bytes 8668160 | tf_op jit(solution)/shard_map/while/body/eval_jaxpr/jvp()/dot_general | solution.py:15
  131.4 4.2 %fusion.73 = f32[256,16]{0,1:T(8,128)S(1)} fusion(f32[16,4096]{1,0:T(8,128)S(1)} %fusion.6, bf16[256,4096]{1,0:T(8,128)(2,1)S(1)} %get-tuple-element.46, f32[256,4096]{1,0:T(8,128)S(1)} %get-tuple-element.42, f32[256]{0:T(256)S(1)} %multiply_multiply_fusion, f32[256]{0:T(256)S(1)} %fusion.61), kind=kOutput, calls=%fused_computation.116 | convolution fusion | flops 207618048 | bytes 6572032 | tf_op jit(solution)/shard_map/while/body/eval_jaxpr/transpose(jvp())/dot_general | solution.py:15
  135.6 2.9 %fusion.9 = bf16[16,4096]{1,0:T(8,128)(2,1)S(1)} fusion(f32[16,4096]{1,0:T(8,128)S(1)} %fusion.6, f32[256,16]{0,1:T(8,128)S(1)} %fusion.15, bf16[16,4096]{1,0:T(8,128)(2,1)S(1)} %reshape.169, bf16[256,4096]{1,0:T(8,128)(2,1)S(1)} %get-tuple-element.46, f32[256,4096]{1,0:T(8,128)S(1)} %get-tuple-element.42, f32[256]{0:T(256)S(1)} %multiply_multiply_fusion, ...), kind=kOutput, calls=%fused_computation.25 | convolution fusion | flops 207945728 | bytes 6834176 | tf_op jit(solution)/shard_map/while/body/eval_jaxpr/transpose(jvp())/dot_general | solution.py:15
  138.5 2.5 fusion.8
  143.4 2.2 reduce.5
  145.8 14.9 %all_to_all.26 = bf16[8,2,8192]{2,1,0:T(2,128)(2,1)S(1)} all-to-all(bf16[8,2,8192]{2,1,0:T(2,128)(2,1)S(1)} %reshape.183), channel_id=1, replica_groups=mesh['head'=8,'client'=4] {'head'}, dimensions={0} | all-to-all | bytes 524288 | tf_op jit(solution)/shard_map/all_to_all | solution.py:84
  162.6 14.3 %all-gather.9.cloned.1.call-done = bf16[1,32,16384]{2,1,0:T(8,128)(2,1)} async-done(((bf16[1,8,16384]{2,1,0:T(8,128)(2,1)}), bf16[1,32,16384]{2,1,0:T(8,128)(2,1)}) %all-gather.9.cloned.1.call-update) | async-done | bytes 1048592 | tf_op jit(solution)/shard_map/all_gather | solution.py:85
  177.0 16.1 %fusion.30 = f32[32,1024]{1,0:T(8,128)} fusion(bf16[1024,16384]{1,0:T(8,128)(2,1)} %param.13, bf16[1,32,16384]{2,1,0:T(8,128)(2,1)} %all-gather.9.cloned.1.call-done), kind=kOutput, calls=%fused_computation.52 | convolution fusion | flops 1073741824 | bytes 34734080 | tf_op jit(solution)/shard_map/dot_general | solution.py:90
  193.1 14.9 %convolution_convert_fusion = bf16[1024,16384]{1,0:T(8,128)(2,1)} fusion(bf16[1,32,16384]{2,1,0:T(8,128)(2,1)S(1)} %copy-done.6, f32[32,1024]{1,0:T(8,128)S(1)} %convolution_add_fusion), kind=kOutput, calls=%fused_computation.1 | convolution fusion | flops 1090584576 | bytes 34734080 | tf_op jit(solution)/shard_map/dot_general | solution.py:87
  207.9 55.7 %all-reduce.2.cloned.1.call-done = f32[32,1024]{1,0:T(8,128)} async-done(((f32[32,1024]{1,0:T(8,128)}), f32[32,1024]{1,0:T(8,128)}) %all-reduce.2.cloned.1.call-update) | async-done | bytes 131088 | tf_op jit(solution)/shard_map/psum | solution.py:95
  263.7 2.5 fusion.42
  (67 shorter events, 18.9 us)
Async XLA Ops:
  7.2 2.5 copy-start
  7.2 52.3 %reduce-scatter.2.cloned.1.call-start = ((), (), s32[]{:S(2)}) async-start(), calls=%async_computation.3 | async-start | bytes 2621440 | tf_op jit(solution)/shard_map/reduce_scatter | solution.py:70
  25.4 58.2 %copy-start.7 = (s32[1,256]{1,0:T(1,128)S(1)}, s32[1,256]{1,0:T(1,128)}, u32[]{:S(2)}) copy-start(s32[1,256]{1,0:T(1,128)} %param.14) | copy-start | bytes 3076
  25.4 58.2 %all-gather.5.cloned.1.call-start = ((), (), s32[]{:S(2)}) async-start(), calls=%async_computation.4 | async-start | bytes 2621440 | tf_op jit(solution)/shard_map/all_gather | solution.py:62
  26.2 81.6 %all-gather.7.cloned.1.call-start = ((), (), s32[]{:S(2)}) async-start(), calls=%async_computation.5 | async-start | bytes 2621440 | tf_op jit(solution)/shard_map/all_gather | solution.py:63
  62.8 25.2 %all-to-all-start = ((bf16[8,2,8192]{2,1,0:T(2,128)(2,1)}), bf16[8,2,8192]{2,1,0:T(2,128)(2,1)S(1)}, u32[]{:S(2)}, u32[]{:S(2)}) async-start(bf16[8,2,8192]{2,1,0:T(2,128)(2,1)} %reshape.181), calls=%async_computation.1 | async-start | bytes 524288 | tf_op jit(solution)/shard_map/all_to_all | solution.py:76
  68.3 108.7 %all-gather.9.cloned.1.call-start = ((), (), s32[]{:S(2)}) async-start(), calls=%async_computation.7 | async-start | bytes 1310720 | tf_op jit(solution)/shard_map/all_gather | solution.py:85
  91.2 5.1 %copy-start.2 = (f32[256,4096]{1,0:T(8,128)S(1)}, f32[256,4096]{1,0:T(8,128)}, u32[]{:S(2)}) copy-start(f32[256,4096]{1,0:T(8,128)} %get-tuple-element.34) | copy-start | bytes 12582916
  100.6 11.1 %copy-start.8 = (s32[1,256]{1,0:T(1,128)S(1)}, s32[1,256]{1,0:T(1,128)}, u32[]{:S(2)}) copy-start(s32[1,256]{1,0:T(1,128)} %param.15) | copy-start | bytes 3076
  107.8 4.6 %copy-start.4 = (f32[256,4096]{1,0:T(8,128)S(1)}, f32[256,4096]{1,0:T(8,128)}, u32[]{:S(2)}) copy-start(f32[256,4096]{1,0:T(8,128)} %get-tuple-element.36) | copy-start | bytes 12582916
  107.8 4.7 %copy-start.5 = (bf16[256,4096]{1,0:T(8,128)(2,1)S(1)}, bf16[256,4096]{1,0:T(8,128)(2,1)}, u32[]{:S(2)}) copy-start(bf16[256,4096]{1,0:T(8,128)(2,1)} %all-gather.7.cloned.1.call-done) | copy-start | bytes 6291460
  116.3 3.1 %copy-start.3 = (f32[256,4096]{1,0:T(8,128)S(1)}, f32[256,4096]{1,0:T(8,128)}, u32[]{:S(2)}) copy-start(f32[256,4096]{1,0:T(8,128)} %get-tuple-element.34) | copy-start | bytes 12582916
  162.0 101.7 %all-reduce.2.cloned.1.call-start = ((), (), s32[]{:S(2)}) async-start(), calls=%async_computation.6 | async-start | bytes 262144 | tf_op jit(solution)/shard_map/psum | solution.py:95
  177.0 16.1 %copy-start.6 = (bf16[1,32,16384]{2,1,0:T(8,128)(2,1)S(1)}, bf16[1,32,16384]{2,1,0:T(8,128)(2,1)}, u32[]{:S(2)}) copy-start(bf16[1,32,16384]{2,1,0:T(8,128)(2,1)} %all-gather.9.cloned.1.call-done) | copy-start | bytes 3145732
  193.1 73.1 %copy-start.1 = (bf16[256,1024]{1,0:T(8,128)(2,1)S(1)}, bf16[256,1024]{1,0:T(8,128)(2,1)}, u32[]{:S(2)}) copy-start(bf16[256,1024]{1,0:T(8,128)(2,1)} %param.11) | copy-start | bytes 1572868
Sparse Core Ops, SparseCore 0:
  25.6 33.9 reduce-scatter.1
  61.1 22.5 all-gather.4
  85.2 22.5 all-gather.6
  162.1 14.7 all-gather.8
  193.2 70.4 all-reduce.1
where the time goes:
time: 278 us; the launch traced here: 274 us
  waiting for transfers between devices  127 us (46%)
  matrix products  95 us (34%)
  between operations  15.9 us (6%)
  blocking collectives  14.9 us (5%)
  local copies, waits for them, and re-layouts  10.8 us (4%)
  starting transfers between devices  5.69 us (2%)
  other arithmetic  5.08 us (2%)
    psum x1, waiting for transfers between devices, local(): hidden_back = lax.psum(hidden_back, 'head')  55.7 us
    reduce_scatter x1, waiting for transfers between devices, local(): lax.psum_scatter(jnp.dot(hidden_rows, head_weight, preferred_element_type...  32.6 us
    dot_general x6, matrix products, client_loss(): jnp.dot(low_rank, factor_b, precision=lax.Precision.HIGHEST)  21.5 us
    dot_general x1, matrix products, local(): lax.dot_general(received, head_weight, (((1,), (1,)), ((), ())), preferre...  16.1 us
    all_gather x1, waiting for transfers between devices, local(): lax.all_gather(byte_table, 'client', axis=1, tiled=True)  15.3 us
    all_to_all x1, blocking collectives, local(): lax.all_to_all(deltas, 'head', split_axis=1, concat_axis=0, tiled=True)  14.9 us
    dot_general x1, matrix products, local(): lax.dot_general(hidden_rows, received, (((0,), (0,)), ((), ())), preferre...  14.9 us
    dot_general x1, matrix products, local(): jnp.dot(hidden_rows, head_weight, preferred_element_type=jnp.float32)  14.9 us
  transfers between devices with their start and end apart: 6, of which 5 were waited for; matrix products, arithmetic and copies ran while one was open for 13% of the time, Pallas kernels for 0%

commit v1 on v0

--- a/solution.py
+++ b/solution.py
@@ -5,6 +5,38 @@
 
 EPSILON = 1e-06
 learn_rate = 0.1
+
+
+def strips_all_feed(my_data, dimension_no, inner_x):
+    part_next = my_data.shape
+    spare = my_data.reshape(
+        *part_next[:dimension_no],
+        inner_x,
+        part_next[dimension_no] // inner_x,
+        *part_next[dimension_no + 1 :]
+    )
+    return jnp.moveaxis(spare, dimension_no, 0)
+
+
+def spots_bind(tile_in, at_axis):
+    tile_in = jnp.moveaxis(tile_in, 0, at_axis)
+    m_next = tile_in.shape
+    return tile_in.reshape(
+        *m_next[:at_axis], m_next[at_axis] * m_next[at_axis + 1], *m_next[at_axis + 2 :]
+    )
+
+
+def part_widths(obj, ax_name, arr_in, array_here):
+    aux, tall = (jax.lax.axis_size(ax_name), jax.lax.axis_index(ax_name))
+    moved = strips_all_feed(obj, arr_in, aux)
+    all_blocks = [moved[tall]]
+    for m in tuple(range(1, aux)):
+        last = moved[(tall + m) % aux]
+        all_blocks.append(
+            jax.lax.ppermute(last, axis_name=ax_name, perm=[(d, (d + m) % aux) for d in range(aux)])
+        )
+    moved = jnp.stack(all_blocks)[(tall - jnp.arange(aux)) % aux]
+    return spots_bind(moved, array_here)
 
 
 def client_loss(factor_a, factor_b, inputs, label_row, out_table):
@@ -81,7 +113,7 @@
         return train_client(record[0], record[1], record[2], byte_full, out_full)
 
     deltas, losses = lax.map(run_client, (owned, tokens, labels))
-    returned = lax.all_to_all(deltas, "head", split_axis=1, concat_axis=0, tiled=True)
+    returned = part_widths(deltas, "head", 1, 0)
     received = lax.all_gather(returned, "client", axis=0, tiled=True)
     hidden_rows = hidden
     grad_sum = lax.dot_general(

time: 278 us -> 281 us (1.011)
  blocking collectives: 14.9 us -> 0 us
  starting transfers between devices: 5.69 us -> 17.2 us
  waiting for transfers between devices: 127 us -> 131 us
    all_to_all x1 -> x0, blocking collectives: 14.9 us -> none  [local(): lax.all_to_all(deltas, 'head', split_axis=1, concat_axis=0, tiled=True)]
    ppermute x0 -> x7, starting transfers between devices: none -> 11.5 us  [part_widths(): jax.lax.ppermute(last, axis_name=ax_name, perm=[(d, (d + m) % aux) for d...]
    ppermute x0 -> x7, waiting for transfers between devices: none -> 4.89 us  [part_widths(): jax.lax.ppermute(last, axis_name=ax_name, perm=[(d, (d + m) % aux) for d...]
    squeeze x0 -> x2, other arithmetic: none -> 3.25 us  [part_widths(): last = moved[(tall + m) % aux]]
  transfers between devices with their start and end apart: 6 -> 13, of which waited for: 5 -> 8; matrix products, arithmetic and copies ran while one was open for 13% -> 14% of each run, Pallas kernels for 0% -> 0%
where the time goes in v1:
time: 281 us; the launch traced here: 277 us
  waiting for transfers between devices  131 us (47%)
  matrix products  95 us (34%)
  starting transfers between devices  17.2 us (6%)
  between operations  16.1 us (6%)
  local copies, waits for them, and re-layouts  11.2 us (4%)
  other arithmetic  6.01 us (2%)
    psum x1, waiting for transfers between devices, local(): hidden_back = lax.psum(hidden_back, 'head')  55.7 us
    reduce_scatter x1, waiting for transfers between devices, local(): lax.psum_scatter(jnp.dot(hidden_rows, head_weight, preferred_element_type...  32.4 us
    dot_general x6, matrix products, client_loss(): jnp.dot(low_rank, factor_b, precision=lax.Precision.HIGHEST)  21.5 us
    dot_general x1, matrix products, local(): lax.dot_general(received, head_weight, (((1,), (1,)), ((), ())), preferre...  16.1 us
    all_gather x1, waiting for transfers between devices, local(): lax.all_gather(byte_table, 'client', axis=1, tiled=True)  15.3 us
    dot_general x1, matrix products, local(): lax.dot_general(hidden_rows, received, (((0,), (0,)), ((), ())), preferre...  14.9 us
    dot_general x1, matrix products, local(): jnp.dot(hidden_rows, head_weight, preferred_element_type=jnp.float32)  14.9 us
    all_gather x1, waiting for transfers between devices, local(): received = lax.all_gather(returned, 'client', axis=0, tiled=True)  14 us
  transfers between devices with their start and end apart: 13, of which 8 were waited for; matrix products, arithmetic and copies ran while one was open for 14% of the time, Pallas kernels for 0%

profile of v1, /device:TPU:0, one launch (start us, length us, event | category | flops | bytes accessed | tf_op | source)
XLA Modules:
  0.0 276.6 jit_solution(5604636575862291413)
XLA Ops:
  10.5 14.9 %fusion.71 = f32[32,16384]{1,0:T(8,128)} fusion(bf16[1024,16384]{1,0:T(8,128)(2,1)} %param.13, f32[32,1024]{1,0:T(8,128)S(1)} %convolution_add_fusion), kind=kOutput, calls=%fused_computation.119 | convolution fusion | flops 1073807360 | bytes 35782656 | tf_op jit(solution)/shard_map/dot_general | solution.py:103
  27.1 32.4 %reduce-scatter.2.cloned.1.call-done = f32[8,16384]{1,0:T(8,128)} async-done(((f32[32,16384]{1,0:T(8,128)}), f32[8,16384]{1,0:T(8,128)}) %reduce-scatter.2.cloned.1.call-update) | async-done | bytes 524304 | tf_op jit(solution)/shard_map/reduce_scatter | solution.py:102
  62.8 5.5 %all-to-all-start = ((bf16[8,2,8192]{2,1,0:T(2,128)(2,1)}), bf16[8,2,8192]{2,1,0:T(2,128)(2,1)S(1)}, u32[]{:S(2)}, u32[]{:S(2)}) async-start(bf16[8,2,8192]{2,1,0:T(2,128)(2,1)} %reshape.235), calls=%async_computation.1 | async-start | bytes 524288 | tf_op jit(solution)/shard_map/all_to_all | solution.py:108
  68.3 15.3 %all-gather.5.cloned.1.call-done = bf16[256,4096]{1,0:T(8,128)(2,1)} async-done(((bf16[256,1024]{1,0:T(8,128)(2,1)}), bf16[256,4096]{1,0:T(8,128)(2,1)}) %all-gather.5.cloned.1.call-update) | async-done | bytes 2097168 | tf_op jit(solution)/shard_map/all_gather | solution.py:94
  83.7 4.4 %multiply_reduce_fusion.2 = (f32[256]{0:T(256)S(1)}, f32[256,4096]{1,0:T(8,128)}) fusion(bf16[256,4096]{1,0:T(8,128)(2,1)} %all-gather.5.cloned.1.call-done, s32[256]{0:T(256)S(1)} %bitcast.66), kind=kOutput, calls=%fused_computation.35 | convolution fusion | flops 539033344 | bytes 6293504 | tf_op jit(solution)/shard_map/while/body/eval_jaxpr/dot_general | solution.py:73
  91.2 5.0 %fusion.18 = f32[256,16]{0,1:T(8,128)S(1)} fusion(bf16[4096,16]{1,0:T(8,128)(2,1)S(1)} %reshape.211, f32[256,4096]{1,0:T(8,128)} %get-tuple-element.42, f32[256]{0:T(256)S(1)} %add_rsqrt_fusion), kind=kOutput, calls=%fused_computation.40 | convolution fusion | flops 202375168 | bytes 4342784 | tf_op jit(solution)/shard_map/while/body/eval_jaxpr/jvp()/dot_general | solution.py:46
  96.3 4.3 %multiply_reduce_fusion.1 = (f32[256]{0:T(256)S(1)}, f32[256,4096]{1,0:T(8,128)}) fusion(f32[256,4096]{1,0:T(8,128)S(1)} %copy-done.2, f32[256,16]{0,1:T(8,128)S(1)} %fusion.18, bf16[16,4096]{1,0:T(8,128)(2,1)S(1)} %reshape.212), kind=kOutput, calls=%fused_computation.34 | convolution fusion | flops 205520640 | bytes 8537088 | tf_op jit(solution)/shard_map/while/body/eval_jaxpr/jvp()/dot_general | solution.py:47
  100.6 7.2 %all-gather.7.cloned.1.call-done = bf16[256,4096]{1,0:T(8,128)(2,1)} async-done(((bf16[256,1024]{1,0:T(8,128)(2,1)}), bf16[256,4096]{1,0:T(8,128)(2,1)}) %all-gather.7.cloned.1.call-update) | async-done | bytes 2097168 | tf_op jit(solution)/shard_map/all_gather | solution.py:95
  107.8 3.9 %fusion.92 = (f32[256]{0:T(256)S(1)}, f32[256,256]{0,1:T(8,128)S(1)}) fusion(bf16[256,4096]{1,0:T(8,128)(2,1)} %all-gather.7.cloned.1.call-done, f32[256,4096]{1,0:T(8,128)} %get-tuple-element.44, f32[256]{0:T(256)S(1)} %fusion.72), kind=kOutput, calls=%fused_computation.153 | convolution fusion | flops 539098880 | bytes 6555648 | tf_op jit(solution)/shard_map/while/body/eval_jaxpr/jvp()/dot_general | solution.py:53
  113.5 2.8 %fusion.90 = f32[256,16]{0,1:T(8,128)S(1)} fusion(bf16[16,4096]{1,0:T(8,128)(2,1)S(1)} %reshape.212, bf16[256,4096]{1,0:T(8,128)(2,1)S(1)} %get-tuple-element.48, f32[256,4096]{1,0:T(8,128)S(1)} %copy-done.4, f32[256]{0:T(256)S(1)} %multiply_multiply_fusion.1, f32[256]{0:T(256)S(1)} %fusion.72), kind=kOutput, calls=%fused_computation.152 | convolution fusion | flops 207618048 | bytes 6440960 | tf_op jit(solution)/shard_map/while/body/eval_jaxpr/transpose(jvp())/dot_general | solution.py:47
  116.3 3.1 %fusion.6 = f32[16,4096]{1,0:T(8,128)S(1)} fusion(f32[256,16]{0,1:T(8,128)S(1)} %fusion.18, bf16[16,4096]{1,0:T(8,128)(2,1)S(1)} %reshape.212, bf16[256,4096]{1,0:T(8,128)(2,1)S(1)} %get-tuple-element.48, f32[256,4096]{1,0:T(8,128)S(1)} %copy-done.4, f32[256]{0:T(256)S(1)} %multiply_multiply_fusion.1, f32[256]{0:T(256)S(1)} %fusion.72), kind=kOutput, calls=%fused_computation.22 | convolution fusion | flops 207814656 | bytes 6703104 | tf_op jit(solution)/shard_map/while/body/eval_jaxpr/transpose(jvp())/dot_general | solution.py:47
  119.4 2.5 fusion.7
  121.9 3.4 %fusion.15 = f32[256,16]{0,1:T(8,128)S(1)} fusion(f32[4096,16]{0,1:T(8,128)S(1)} %fusion.7, f32[256,4096]{1,0:T(8,128)S(1)} %copy-done.3, f32[256]{0:T(256)S(1)} %add_rsqrt_fusion), kind=kOutput, calls=%fused_computation.37 | convolution fusion | flops 202375168 | bytes 4473856 | tf_op jit(solution)/shard_map/while/body/eval_jaxpr/jvp()/dot_general | solution.py:46
  125.4 4.1 %multiply_reduce_fusion = (f32[256]{0:T(256)S(1)}, f32[256,4096]{1,0:T(8,128)S(1)}) fusion(f32[256,4096]{1,0:T(8,128)S(1)} %copy-done.3, f32[256,16]{0,1:T(8,128)S(1)} %fusion.15, f32[16,4096]{1,0:T(8,128)S(1)} %fusion.6), kind=kOutput, calls=%fused_computation.32 | convolution fusion | flops 205520640 | bytes 8668160 | tf_op jit(solution)/shard_map/while/body/eval_jaxpr/jvp()/dot_general | solution.py:47
  131.4 4.2 %fusion.87 = f32[256,16]{0,1:T(8,128)S(1)} fusion(f32[16,4096]{1,0:T(8,128)S(1)} %fusion.6, bf16[256,4096]{1,0:T(8,128)(2,1)S(1)} %get-tuple-element.54, f32[256,4096]{1,0:T(8,128)S(1)} %get-tuple-element.50, f32[256]{0:T(256)S(1)} %multiply_multiply_fusion, f32[256]{0:T(256)S(1)} %fusion.73), kind=kOutput, calls=%fused_computation.151 | convolution fusion | flops 207618048 | bytes 6572032 | tf_op jit(solution)/shard_map/while/body/eval_jaxpr/transpose(jvp())/dot_general | solution.py:47
  135.6 2.9 %fusion.9 = bf16[16,4096]{1,0:T(8,128)(2,1)S(1)} fusion(f32[16,4096]{1,0:T(8,128)S(1)} %fusion.6, f32[256,16]{0,1:T(8,128)S(1)} %fusion.15, bf16[16,4096]{1,0:T(8,128)(2,1)S(1)} %reshape.212, bf16[256,4096]{1,0:T(8,128)(2,1)S(1)} %get-tuple-element.54, f32[256,4096]{1,0:T(8,128)S(1)} %get-tuple-element.50, f32[256]{0:T(256)S(1)} %multiply_multiply_fusion, ...), kind=kOutput, calls=%fused_computation.26 | convolution fusion | flops 207945728 | bytes 6834176 | tf_op jit(solution)/shard_map/while/body/eval_jaxpr/transpose(jvp())/dot_general | solution.py:47
  138.5 2.5 fusion.8
  143.4 3.4 %collective-permute-start.4 = (bf16[1,16384]{1,0:T(2,128)(2,1)S(1)}, bf16[1,16384]{1,0:T(2,128)(2,1)S(1)}, u32[]{:S(2)}, u32[]{:S(2)}) collective-permute-start(bf16[1,16384]{1,0:T(2,128)(2,1)S(1)} %get-tuple-element.38), channel_id=1, source_target_pairs={{0,20},{4,24},{8,28},{12,0},{16,4},{20,8},{24,12},{28,16},{1,21},{... | collective-permute-start | bytes 98312 | tf_op jit(solution)/shard_map/ppermute | solution.py:36
  148.4 2.8 fusion.70
  152.8 2.8 %collective-permute-start.6 = (bf16[1,16384]{1,0:T(2,128)(2,1)S(1)}, bf16[1,16384]{1,0:T(2,128)(2,1)S(1)}, u32[]{:S(2)}, u32[]{:S(2)}) collective-permute-start(bf16[1,16384]{1,0:T(2,128)(2,1)S(1)} %get-tuple-element.23), channel_id=1, source_target_pairs={{0,28},{4,0},{8,4},{12,8},{16,12},{20,16},{24,20},{28,24},{1,29},{... | collective-permute-start | bytes 98312 | tf_op jit(solution)/shard_map/ppermute | solution.py:36
  165.5 14.0 %all-gather.9.cloned.1.call-done = bf16[32,16384]{1,0:T(8,128)(2,1)} async-done(((bf16[8,16384]{1,0:T(8,128)(2,1)}), bf16[32,16384]{1,0:T(8,128)(2,1)}) %all-gather.9.cloned.1.call-update) | async-done | bytes 1048592 | tf_op jit(solution)/shard_map/all_gather | solution.py:117
  179.5 16.1 %fusion.94 = f32[32,1024]{1,0:T(8,128)} fusion(bf16[32,16384]{1,0:T(8,128)(2,1)} %all-gather.9.cloned.1.call-done, bf16[1024,16384]{1,0:T(8,128)(2,1)} %param.13), kind=kOutput, calls=%fused_computation.155 | convolution fusion | flops 1073741824 | bytes 34734080 | tf_op jit(solution)/shard_map/dot_general | solution.py:122
  195.6 14.9 %convolution_convert_fusion = bf16[1024,16384]{1,0:T(8,128)(2,1)} fusion(bf16[32,16384]{1,0:T(8,128)(2,1)S(1)} %copy-done.6, f32[32,1024]{1,0:T(8,128)S(1)} %convolution_add_fusion), kind=kOutput, calls=%fused_computation.2 | convolution fusion | flops 1090584576 | bytes 34734080 | tf_op jit(solution)/shard_map/dot_general | solution.py:119
  210.5 55.7 %all-reduce.2.cloned.1.call-done = f32[32,1024]{1,0:T(8,128)} async-done(((f32[32,1024]{1,0:T(8,128)}), f32[32,1024]{1,0:T(8,128)}) %all-reduce.2.cloned.1.call-update) | async-done | bytes 131088 | tf_op jit(solution)/shard_map/psum | solution.py:127
  (80 shorter events, 32.4 us)
Async XLA Ops:
  7.2 2.5 copy-start
  7.2 52.3 %reduce-scatter.2.cloned.1.call-start = ((), (), s32[]{:S(2)}) async-start(), calls=%async_computation.2 | async-start | bytes 2621440 | tf_op jit(solution)/shard_map/reduce_scatter | solution.py:102
  25.4 58.2 %copy-start.7 = (s32[1,256]{1,0:T(1,128)S(1)}, s32[1,256]{1,0:T(1,128)}, u32[]{:S(2)}) copy-start(s32[1,256]{1,0:T(1,128)} %param.14) | copy-start | bytes 3076
  25.4 58.2 %all-gather.5.cloned.1.call-start = ((), (), s32[]{:S(2)}) async-start(), calls=%async_computation.3 | async-start | bytes 2621440 | tf_op jit(solution)/shard_map/all_gather | solution.py:94
  26.2 81.6 %all-gather.7.cloned.1.call-start = ((), (), s32[]{:S(2)}) async-start(), calls=%async_computation.4 | async-start | bytes 2621440 | tf_op jit(solution)/shard_map/all_gather | solution.py:95
  62.8 25.2 %all-to-all-start = ((bf16[8,2,8192]{2,1,0:T(2,128)(2,1)}), bf16[8,2,8192]{2,1,0:T(2,128)(2,1)S(1)}, u32[]{:S(2)}, u32[]{:S(2)}) async-start(bf16[8,2,8192]{2,1,0:T(2,128)(2,1)} %reshape.235), calls=%async_computation.1 | async-start | bytes 524288 | tf_op jit(solution)/shard_map/all_to_all | solution.py:108
  68.3 111.2 %all-gather.9.cloned.1.call-start = ((), (), s32[]{:S(2)}) async-start(), calls=%async_computation.6 | async-start | bytes 1310720 | tf_op jit(solution)/shard_map/all_gather | solution.py:117
  91.2 5.1 %copy-start.2 = (f32[256,4096]{1,0:T(8,128)S(1)}, f32[256,4096]{1,0:T(8,128)}, u32[]{:S(2)}) copy-start(f32[256,4096]{1,0:T(8,128)} %get-tuple-element.42) | copy-start | bytes 12582916
  100.6 11.1 %copy-start.8 = (s32[1,256]{1,0:T(1,128)S(1)}, s32[1,256]{1,0:T(1,128)}, u32[]{:S(2)}) copy-start(s32[1,256]{1,0:T(1,128)} %param.15) | copy-start | bytes 3076
  107.8 4.6 %copy-start.4 = (f32[256,4096]{1,0:T(8,128)S(1)}, f32[256,4096]{1,0:T(8,128)}, u32[]{:S(2)}) copy-start(f32[256,4096]{1,0:T(8,128)} %get-tuple-element.44) | copy-start | bytes 12582916
  107.8 4.7 %copy-start.5 = (bf16[256,4096]{1,0:T(8,128)(2,1)S(1)}, bf16[256,4096]{1,0:T(8,128)(2,1)}, u32[]{:S(2)}) copy-start(bf16[256,4096]{1,0:T(8,128)(2,1)} %all-gather.7.cloned.1.call-done) | copy-start | bytes 6291460
  116.3 3.1 %copy-start.3 = (f32[256,4096]{1,0:T(8,128)S(1)}, f32[256,4096]{1,0:T(8,128)}, u32[]{:S(2)}) copy-start(f32[256,4096]{1,0:T(8,128)} %get-tuple-element.42) | copy-start | bytes 12582916
  143.4 12.2 %collective-permute-start.4 = (bf16[1,16384]{1,0:T(2,128)(2,1)S(1)}, bf16[1,16384]{1,0:T(2,128)(2,1)S(1)}, u32[]{:S(2)}, u32[]{:S(2)}) collective-permute-start(bf16[1,16384]{1,0:T(2,128)(2,1)S(1)} %get-tuple-element.38), channel_id=1, source_target_pairs={{0,20},{4,24},{8,28},{12,0},{16,4},{20,8},{24,12},{28,16},{1,21},{... | collective-permute-start | bytes 98312 | tf_op jit(solution)/shard_map/ppermute | solution.py:36
  146.8 8.9 %collective-permute-start.5 = (bf16[1,16384]{1,0:T(2,128)(2,1)S(1)}, bf16[1,16384]{1,0:T(2,128)(2,1)S(1)}, u32[]{:S(2)}, u32[]{:S(2)}) collective-permute-start(bf16[1,16384]{1,0:T(2,128)(2,1)S(1)} %get-tuple-element.37), channel_id=1, source_target_pairs={{0,24},{4,28},{8,0},{12,4},{16,8},{20,12},{24,16},{28,20},{1,25},{... | collective-permute-start | bytes 98312 | tf_op jit(solution)/shard_map/ppermute | solution.py:36
  151.2 8.5 %collective-permute-start.2 = (bf16[1,16384]{1,0:T(2,128)(2,1)S(1)}, bf16[1,16384]{1,0:T(2,128)(2,1)S(1)}, u32[]{:S(2)}, u32[]{:S(2)}) collective-permute-start(bf16[1,16384]{1,0:T(2,128)(2,1)S(1)} %get-tuple-element.35), channel_id=1, source_target_pairs={{0,12},{4,16},{8,20},{12,24},{16,28},{20,0},{24,4},{28,8},{1,13},{... | collective-permute-start | bytes 98312 | tf_op jit(solution)/shard_map/ppermute | solution.py:36
  152.8 7.6 %collective-permute-start.3 = (bf16[1,16384]{1,0:T(2,128)(2,1)S(1)}, bf16[1,16384]{1,0:T(2,128)(2,1)S(1)}, u32[]{:S(2)}, u32[]{:S(2)}) collective-permute-start(bf16[1,16384]{1,0:T(2,128)(2,1)S(1)} %get-tuple-element.36), channel_id=1, source_target_pairs={{0,16},{4,20},{8,24},{12,28},{16,0},{20,4},{24,8},{28,12},{1,17},{... | collective-permute-start | bytes 98312 | tf_op jit(solution)/shard_map/ppermute | solution.py:36
  152.8 7.5 %collective-permute-start.6 = (bf16[1,16384]{1,0:T(2,128)(2,1)S(1)}, bf16[1,16384]{1,0:T(2,128)(2,1)S(1)}, u32[]{:S(2)}, u32[]{:S(2)}) collective-permute-start(bf16[1,16384]{1,0:T(2,128)(2,1)S(1)} %get-tuple-element.23), channel_id=1, source_target_pairs={{0,28},{4,0},{8,4},{12,8},{16,12},{20,16},{24,20},{28,24},{1,29},{... | collective-permute-start | bytes 98312 | tf_op jit(solution)/shard_map/ppermute | solution.py:36
  155.6 7.0 %collective-permute-start = (bf16[1,16384]{1,0:T(2,128)(2,1)S(1)}, bf16[1,16384]{1,0:T(2,128)(2,1)S(1)}, u32[]{:S(2)}, u32[]{:S(2)}) collective-permute-start(bf16[1,16384]{1,0:T(2,128)(2,1)S(1)} %get-tuple-element.33), channel_id=1, source_target_pairs={{0,4},{4,8},{8,12},{12,16},{16,20},{20,24},{24,28},{28,0},{1,5},{5... | collective-permute-start | bytes 98312 | tf_op jit(solution)/shard_map/ppermute | solution.py:36
  155.6 6.9 %collective-permute-start.1 = (bf16[1,16384]{1,0:T(2,128)(2,1)S(1)}, bf16[1,16384]{1,0:T(2,128)(2,1)S(1)}, u32[]{:S(2)}, u32[]{:S(2)}) collective-permute-start(bf16[1,16384]{1,0:T(2,128)(2,1)S(1)} %get-tuple-element.34), channel_id=1, source_target_pairs={{0,8},{4,12},{8,16},{12,20},{16,24},{20,28},{24,0},{28,4},{1,9},{5... | collective-permute-start | bytes 98312 | tf_op jit(solution)/shard_map/ppermute | solution.py:36
  164.8 101.4 %all-reduce.2.cloned.1.call-start = ((), (), s32[]{:S(2)}) async-start(), calls=%async_computation.5 | async-start | bytes 262144 | tf_op jit(solution)/shard_map/psum | solution.py:127
  179.5 16.1 %copy-start.6 = (bf16[32,16384]{1,0:T(8,128)(2,1)S(1)}, bf16[32,16384]{1,0:T(8,128)(2,1)}, u32[]{:S(2)}) copy-start(bf16[32,16384]{1,0:T(8,128)(2,1)} %all-gather.9.cloned.1.call-done) | copy-start | bytes 3145732
  195.6 73.1 %copy-start.1 = (bf16[256,1024]{1,0:T(8,128)(2,1)S(1)}, bf16[256,1024]{1,0:T(8,128)(2,1)}, u32[]{:S(2)}) copy-start(bf16[256,1024]{1,0:T(8,128)(2,1)} %param.11) | copy-start | bytes 1572868
Sparse Core Ops, SparseCore 0:
  25.6 33.9 reduce-scatter.1
  61.1 22.5 all-gather.4
  85.2 22.5 all-gather.6
  165.0 14.5 all-gather.8
  195.7 70.4 all-reduce.1
